TPU v7x, 64 devices: a 2x2x8 block of a 4x4x8 slice. The times are simulated.
64 devices in a mesh: dp: 4 (over x, y), tp: 16 (over z, core).
Axes of the slice: x: 2, y: 2, z: 8, core: 2. Of those that a mesh axis runs over, the one named last changes fastest.
The devices are a block of a 4x4x8 slice.
Arguments:
- hidden: bfloat16 [32768, 2048], P(('dp', 'tp')), parts along dimension 0
- norm_scale: float32 [2048], replicated
- embed: bfloat16 [151936, 2048], P('tp')
- target: int32 [32768], P(('dp', 'tp')), parts along dimension 0
Outputs:
- output 1: float32 [32768], P(('dp', 'tp')), parts along dimension 0
- output 2: float32 [32768], P(('dp', 'tp')), parts along dimension 0
There are 4 independent parts. A program takes and returns all parts, laid end to end along the dimension named above; an argument that names none is the same for every part.
All inputs are finite; a program needn't handle non-finite values.
Results may differ from a plain program's by a relative error of at most 0.001.
Values are sent between devices in bfloat16 or wider.
A program may use at most 768 MiB of HBM per device.

v0:
```python
import jax
import jax.numpy as jnp
from jax import lax
from jax.sharding import PartitionSpec as P

NORM_EPS = 1e-5
OUT_SCALE = 0.5773502691896257


def rms_norm(hidden, norm_scale):
    rows = hidden.astype(jnp.float32)
    mean_sq = jnp.mean(rows * rows, axis=-1, keepdims=True)
    return (rows * lax.rsqrt(mean_sq + NORM_EPS) * norm_scale).astype(jnp.bfloat16)


def shard_stats(normed, table, local_ids):
    logits = jnp.einsum("td,vd->tv", normed, table, preferred_element_type=jnp.float32) * OUT_SCALE
    row_max = jnp.max(logits, axis=-1)
    exp_sum = jnp.sum(jnp.exp(logits - row_max[:, None]), axis=-1)
    vocab_pos = jnp.arange(table.shape[0], dtype=jnp.int32)
    tgt_logit = jnp.sum(jnp.where(vocab_pos[None, :] == local_ids[:, None], logits, 0.0), axis=-1)
    return row_max, exp_sum, tgt_logit


def solution(mesh):
    row_spec = P(("dp", "tp"))

    def local_part(hidden, norm_scale, embed, target):
        shard_idx = lax.axis_index("tp")
        shard_rows = embed.shape[0]
        normed = rms_norm(hidden, norm_scale)
        all_rows = lax.all_gather(normed, "tp")
        all_ids = lax.all_gather(target, "tp") - shard_idx * shard_rows

        def one_block(block):
            block_rows, block_ids = block
            return jnp.stack(shard_stats(block_rows, embed, block_ids))

        tok_stats = lax.map(one_block, (all_rows, all_ids))
        tok_stats = lax.all_to_all(tok_stats, "tp", 0, 0, tiled=True)
        glob_max = jnp.max(tok_stats[:, 0], axis=0)
        total = jnp.sum(tok_stats[:, 1] * jnp.exp(tok_stats[:, 0] - glob_max), axis=0)
        log_sum = glob_max + jnp.log(total)
        return jnp.sum(tok_stats[:, 2], axis=0) - log_sum, log_sum

    return jax.shard_map(local_part, mesh=mesh,
                         in_specs=(P(("dp", "tp"), None), P(None), P("tp", None), row_spec),
                         out_specs=(row_spec, row_spec), check_vma=False)
```

profile of v0, /device:TPU:21, one launch (start us, length us, event | category | flops | bytes accessed | tf_op | source)
XLA Modules:
  0.0 830.2 jit_solution(6405291427561130295)
XLA Ops:
  12.9 22.9 %all-gather.2 = s32[16,1,512]{2,1,0:T(1,128)S(1)} all-gather(s32[1,1,512]{2,1,0:T(1,128)} %bitcast.54), channel_id=3, replica_groups=mesh['dp'=4,'tp'=16] {'tp'}, dimensions={0}, use_global_device_ids=true | all-gather | bytes 34816 | tf_op jit(solution)/shard_map/all_gather | solution.py:33
  35.8 153.4 %all-gather.5.cloned.1.call-done = bf16[8192,2048]{1,0:T(8,128)(2,1)} async-done(((bf16[512,2048]{1,0:T(8,128)(2,1)}), bf16[8192,2048]{1,0:T(8,128)(2,1)}) %all-gather.5.cloned.1.call-update) | async-done | bytes 33554448 | tf_op jit(solution)/shard_map/all_gather | solution.py:32
  189.1 620.2 %while.10 = (s32[]{:T(128)}, f32[16,3,512]{2,1,0:T(4,128)S(1)}, bf16[16,512,2048]{2,1,0:T(8,128)(2,1)}, bf16[9496,2048]{1,0:T(8,128)(2,1)}, s32[16,512]{1,0:T(8,128)S(1)}, /*index=5*/s32[]{:T(128)}) while((s32[]{:T(128)}, f32[16,3,512]{2,1,0:T(4,128)S(1)}, bf16[16,512,2048]{2,1,0:T(8,128)(2,1)}, bf16[9496,2048]{1,0:T(8,128)(2,1)}, ...), condition=%wide.region_5.6_spmd, body=%wide.region_1.5_spmd.sunk | while | flops 19953455104 | bytes 79917640 | solution.py:39
  189.1 28.9 %multiply_reduce_fusion.2 = (f32[512]{0:T(512)S(1)}, f32[512,9496]{0,1:T(8,128)}) fusion(bf16[9496,2048]{1,0:T(8,128)(2,1)} %get-tuple-element.106, bf16[16,512,2048]{2,1,0:T(8,128)(2,1)} %get-tuple-element.105, s32[]{:T(128)} %get-tuple-element.97), kind=kOutput, calls=%fused_computation.3.clone.1 | convolution fusion | flops 19924279296 | bytes 60443136 | tf_op jit(solution)/shard_map/while/body/eval_jaxpr/td,vd->tv/dot_general | solution.py:17
  218.0 9.8 %exponential_reduce_fusion.2 = (f32[512]{0:T(512)S(1)}, f32[512]{0:T(512)S(1)}) fusion(f32[512,9496]{0,1:T(8,128)} %get-tuple-element.87, f32[512]{0:T(512)S(1)} %get-tuple-element.88, s32[512]{0:T(512)S(1)} %bitcast.47), kind=kLoop, calls=%fused_computation.2.clone.1 | loop fusion | flops 29170688 | bytes 19456000 | tf_op jit(solution)/shard_map/while/body/eval_jaxpr/reduce_sum | solution.py:19
  227.9 28.9 %multiply_reduce_fusion.2 = (f32[512]{0:T(512)S(1)}, f32[512,9496]{0,1:T(8,128)}) fusion(bf16[9496,2048]{1,0:T(8,128)(2,1)} %get-tuple-element.106, bf16[16,512,2048]{2,1,0:T(8,128)(2,1)} %get-tuple-element.105, s32[]{:T(128)} %get-tuple-element.97), kind=kOutput, calls=%fused_computation.3.clone.1 | convolution fusion | flops 19924279296 | bytes 60443136 | tf_op jit(solution)/shard_map/while/body/eval_jaxpr/td,vd->tv/dot_general | solution.py:17
  256.8 9.8 %exponential_reduce_fusion.2 = (f32[512]{0:T(512)S(1)}, f32[512]{0:T(512)S(1)}) fusion(f32[512,9496]{0,1:T(8,128)} %get-tuple-element.87, f32[512]{0:T(512)S(1)} %get-tuple-element.88, s32[512]{0:T(512)S(1)} %bitcast.47), kind=kLoop, calls=%fused_computation.2.clone.1 | loop fusion | flops 29170688 | bytes 19456000 | tf_op jit(solution)/shard_map/while/body/eval_jaxpr/reduce_sum | solution.py:19
  266.6 28.9 %multiply_reduce_fusion.2 = (f32[512]{0:T(512)S(1)}, f32[512,9496]{0,1:T(8,128)}) fusion(bf16[9496,2048]{1,0:T(8,128)(2,1)} %get-tuple-element.106, bf16[16,512,2048]{2,1,0:T(8,128)(2,1)} %get-tuple-element.105, s32[]{:T(128)} %get-tuple-element.97), kind=kOutput, calls=%fused_computation.3.clone.1 | convolution fusion | flops 19924279296 | bytes 60443136 | tf_op jit(solution)/shard_map/while/body/eval_jaxpr/td,vd->tv/dot_general | solution.py:17
  295.5 9.8 %exponential_reduce_fusion.2 = (f32[512]{0:T(512)S(1)}, f32[512]{0:T(512)S(1)}) fusion(f32[512,9496]{0,1:T(8,128)} %get-tuple-element.87, f32[512]{0:T(512)S(1)} %get-tuple-element.88, s32[512]{0:T(512)S(1)} %bitcast.47), kind=kLoop, calls=%fused_computation.2.clone.1 | loop fusion | flops 29170688 | bytes 19456000 | tf_op jit(solution)/shard_map/while/body/eval_jaxpr/reduce_sum | solution.py:19
  305.4 28.9 %multiply_reduce_fusion.2 = (f32[512]{0:T(512)S(1)}, f32[512,9496]{0,1:T(8,128)}) fusion(bf16[9496,2048]{1,0:T(8,128)(2,1)} %get-tuple-element.106, bf16[16,512,2048]{2,1,0:T(8,128)(2,1)} %get-tuple-element.105, s32[]{:T(128)} %get-tuple-element.97), kind=kOutput, calls=%fused_computation.3.clone.1 | convolution fusion | flops 19924279296 | bytes 60443136 | tf_op jit(solution)/shard_map/while/body/eval_jaxpr/td,vd->tv/dot_general | solution.py:17
  334.3 9.8 %exponential_reduce_fusion.2 = (f32[512]{0:T(512)S(1)}, f32[512]{0:T(512)S(1)}) fusion(f32[512,9496]{0,1:T(8,128)} %get-tuple-element.87, f32[512]{0:T(512)S(1)} %get-tuple-element.88, s32[512]{0:T(512)S(1)} %bitcast.47), kind=kLoop, calls=%fused_computation.2.clone.1 | loop fusion | flops 29170688 | bytes 19456000 | tf_op jit(solution)/shard_map/while/body/eval_jaxpr/reduce_sum | solution.py:19
  344.1 28.9 %multiply_reduce_fusion.2 = (f32[512]{0:T(512)S(1)}, f32[512,9496]{0,1:T(8,128)}) fusion(bf16[9496,2048]{1,0:T(8,128)(2,1)} %get-tuple-element.106, bf16[16,512,2048]{2,1,0:T(8,128)(2,1)} %get-tuple-element.105, s32[]{:T(128)} %get-tuple-element.97), kind=kOutput, calls=%fused_computation.3.clone.1 | convolution fusion | flops 19924279296 | bytes 60443136 | tf_op jit(solution)/shard_map/while/body/eval_jaxpr/td,vd->tv/dot_general | solution.py:17
  373.0 9.8 %exponential_reduce_fusion.2 = (f32[512]{0:T(512)S(1)}, f32[512]{0:T(512)S(1)}) fusion(f32[512,9496]{0,1:T(8,128)} %get-tuple-element.87, f32[512]{0:T(512)S(1)} %get-tuple-element.88, s32[512]{0:T(512)S(1)} %bitcast.47), kind=kLoop, calls=%fused_computation.2.clone.1 | loop fusion | flops 29170688 | bytes 19456000 | tf_op jit(solution)/shard_map/while/body/eval_jaxpr/reduce_sum | solution.py:19
  382.9 28.9 %multiply_reduce_fusion.2 = (f32[512]{0:T(512)S(1)}, f32[512,9496]{0,1:T(8,128)}) fusion(bf16[9496,2048]{1,0:T(8,128)(2,1)} %get-tuple-element.106, bf16[16,512,2048]{2,1,0:T(8,128)(2,1)} %get-tuple-element.105, s32[]{:T(128)} %get-tuple-element.97), kind=kOutput, calls=%fused_computation.3.clone.1 | convolution fusion | flops 19924279296 | bytes 60443136 | tf_op jit(solution)/shard_map/while/body/eval_jaxpr/td,vd->tv/dot_general | solution.py:17
  411.8 9.8 %exponential_reduce_fusion.2 = (f32[512]{0:T(512)S(1)}, f32[512]{0:T(512)S(1)}) fusion(f32[512,9496]{0,1:T(8,128)} %get-tuple-element.87, f32[512]{0:T(512)S(1)} %get-tuple-element.88, s32[512]{0:T(512)S(1)} %bitcast.47), kind=kLoop, calls=%fused_computation.2.clone.1 | loop fusion | flops 29170688 | bytes 19456000 | tf_op jit(solution)/shard_map/while/body/eval_jaxpr/reduce_sum | solution.py:19
  421.7 28.9 %multiply_reduce_fusion.2 = (f32[512]{0:T(512)S(1)}, f32[512,9496]{0,1:T(8,128)}) fusion(bf16[9496,2048]{1,0:T(8,128)(2,1)} %get-tuple-element.106, bf16[16,512,2048]{2,1,0:T(8,128)(2,1)} %get-tuple-element.105, s32[]{:T(128)} %get-tuple-element.97), kind=kOutput, calls=%fused_computation.3.clone.1 | convolution fusion | flops 19924279296 | bytes 60443136 | tf_op jit(solution)/shard_map/while/body/eval_jaxpr/td,vd->tv/dot_general | solution.py:17
  450.6 9.8 %exponential_reduce_fusion.2 = (f32[512]{0:T(512)S(1)}, f32[512]{0:T(512)S(1)}) fusion(f32[512,9496]{0,1:T(8,128)} %get-tuple-element.87, f32[512]{0:T(512)S(1)} %get-tuple-element.88, s32[512]{0:T(512)S(1)} %bitcast.47), kind=kLoop, calls=%fused_computation.2.clone.1 | loop fusion | flops 29170688 | bytes 19456000 | tf_op jit(solution)/shard_map/while/body/eval_jaxpr/reduce_sum | solution.py:19
  460.4 28.9 %multiply_reduce_fusion.2 = (f32[512]{0:T(512)S(1)}, f32[512,9496]{0,1:T(8,128)}) fusion(bf16[9496,2048]{1,0:T(8,128)(2,1)} %get-tuple-element.106, bf16[16,512,2048]{2,1,0:T(8,128)(2,1)} %get-tuple-element.105, s32[]{:T(128)} %get-tuple-element.97), kind=kOutput, calls=%fused_computation.3.clone.1 | convolution fusion | flops 19924279296 | bytes 60443136 | tf_op jit(solution)/shard_map/while/body/eval_jaxpr/td,vd->tv/dot_general | solution.py:17
  489.3 9.8 %exponential_reduce_fusion.2 = (f32[512]{0:T(512)S(1)}, f32[512]{0:T(512)S(1)}) fusion(f32[512,9496]{0,1:T(8,128)} %get-tuple-element.87, f32[512]{0:T(512)S(1)} %get-tuple-element.88, s32[512]{0:T(512)S(1)} %bitcast.47), kind=kLoop, calls=%fused_computation.2.clone.1 | loop fusion | flops 29170688 | bytes 19456000 | tf_op jit(solution)/shard_map/while/body/eval_jaxpr/reduce_sum | solution.py:19
  499.2 28.9 %multiply_reduce_fusion.2 = (f32[512]{0:T(512)S(1)}, f32[512,9496]{0,1:T(8,128)}) fusion(bf16[9496,2048]{1,0:T(8,128)(2,1)} %get-tuple-element.106, bf16[16,512,2048]{2,1,0:T(8,128)(2,1)} %get-tuple-element.105, s32[]{:T(128)} %get-tuple-element.97), kind=kOutput, calls=%fused_computation.3.clone.1 | convolution fusion | flops 19924279296 | bytes 60443136 | tf_op jit(solution)/shard_map/while/body/eval_jaxpr/td,vd->tv/dot_general | solution.py:17
  528.1 9.8 %exponential_reduce_fusion.2 = (f32[512]{0:T(512)S(1)}, f32[512]{0:T(512)S(1)}) fusion(f32[512,9496]{0,1:T(8,128)} %get-tuple-element.87, f32[512]{0:T(512)S(1)} %get-tuple-element.88, s32[512]{0:T(512)S(1)} %bitcast.47), kind=kLoop, calls=%fused_computation.2.clone.1 | loop fusion | flops 29170688 | bytes 19456000 | tf_op jit(solution)/shard_map/while/body/eval_jaxpr/reduce_sum | solution.py:19
  538.0 28.9 %multiply_reduce_fusion.2 = (f32[512]{0:T(512)S(1)}, f32[512,9496]{0,1:T(8,128)}) fusion(bf16[9496,2048]{1,0:T(8,128)(2,1)} %get-tuple-element.106, bf16[16,512,2048]{2,1,0:T(8,128)(2,1)} %get-tuple-element.105, s32[]{:T(128)} %get-tuple-element.97), kind=kOutput, calls=%fused_computation.3.clone.1 | convolution fusion | flops 19924279296 | bytes 60443136 | tf_op jit(solution)/shard_map/while/body/eval_jaxpr/td,vd->tv/dot_general | solution.py:17
  566.9 9.8 %exponential_reduce_fusion.2 = (f32[512]{0:T(512)S(1)}, f32[512]{0:T(512)S(1)}) fusion(f32[512,9496]{0,1:T(8,128)} %get-tuple-element.87, f32[512]{0:T(512)S(1)} %get-tuple-element.88, s32[512]{0:T(512)S(1)} %bitcast.47), kind=kLoop, calls=%fused_computation.2.clone.1 | loop fusion | flops 29170688 | bytes 19456000 | tf_op jit(solution)/shard_map/while/body/eval_jaxpr/reduce_sum | solution.py:19
  576.7 28.9 %multiply_reduce_fusion.2 = (f32[512]{0:T(512)S(1)}, f32[512,9496]{0,1:T(8,128)}) fusion(bf16[9496,2048]{1,0:T(8,128)(2,1)} %get-tuple-element.106, bf16[16,512,2048]{2,1,0:T(8,128)(2,1)} %get-tuple-element.105, s32[]{:T(128)} %get-tuple-element.97), kind=kOutput, calls=%fused_computation.3.clone.1 | convolution fusion | flops 19924279296 | bytes 60443136 | tf_op jit(solution)/shard_map/while/body/eval_jaxpr/td,vd->tv/dot_general | solution.py:17
  605.6 9.8 %exponential_reduce_fusion.2 = (f32[512]{0:T(512)S(1)}, f32[512]{0:T(512)S(1)}) fusion(f32[512,9496]{0,1:T(8,128)} %get-tuple-element.87, f32[512]{0:T(512)S(1)} %get-tuple-element.88, s32[512]{0:T(512)S(1)} %bitcast.47), kind=kLoop, calls=%fused_computation.2.clone.1 | loop fusion | flops 29170688 | bytes 19456000 | tf_op jit(solution)/shard_map/while/body/eval_jaxpr/reduce_sum | solution.py:19
  615.5 28.9 %multiply_reduce_fusion.2 = (f32[512]{0:T(512)S(1)}, f32[512,9496]{0,1:T(8,128)}) fusion(bf16[9496,2048]{1,0:T(8,128)(2,1)} %get-tuple-element.106, bf16[16,512,2048]{2,1,0:T(8,128)(2,1)} %get-tuple-element.105, s32[]{:T(128)} %get-tuple-element.97), kind=kOutput, calls=%fused_computation.3.clone.1 | convolution fusion | flops 19924279296 | bytes 60443136 | tf_op jit(solution)/shard_map/while/body/eval_jaxpr/td,vd->tv/dot_general | solution.py:17
  654.2 28.9 %multiply_reduce_fusion.2 = (f32[512]{0:T(512)S(1)}, f32[512,9496]{0,1:T(8,128)}) fusion(bf16[9496,2048]{1,0:T(8,128)(2,1)} %get-tuple-element.106, bf16[16,512,2048]{2,1,0:T(8,128)(2,1)} %get-tuple-element.105, s32[]{:T(128)} %get-tuple-element.97), kind=kOutput, calls=%fused_computation.3.clone.1 | convolution fusion | flops 19924279296 | bytes 60443136 | tf_op jit(solution)/shard_map/while/body/eval_jaxpr/td,vd->tv/dot_general | solution.py:17
  693.0 28.9 %multiply_reduce_fusion.2 = (f32[512]{0:T(512)S(1)}, f32[512,9496]{0,1:T(8,128)}) fusion(bf16[9496,2048]{1,0:T(8,128)(2,1)} %get-tuple-element.106, bf16[16,512,2048]{2,1,0:T(8,128)(2,1)} %get-tuple-element.105, s32[]{:T(128)} %get-tuple-element.97), kind=kOutput, calls=%fused_computation.3.clone.1 | convolution fusion | flops 19924279296 | bytes 60443136 | tf_op jit(solution)/shard_map/while/body/eval_jaxpr/td,vd->tv/dot_general | solution.py:17
  731.8 28.9 %multiply_reduce_fusion.2 = (f32[512]{0:T(512)S(1)}, f32[512,9496]{0,1:T(8,128)}) fusion(bf16[9496,2048]{1,0:T(8,128)(2,1)} %get-tuple-element.106, bf16[16,512,2048]{2,1,0:T(8,128)(2,1)} %get-tuple-element.105, s32[]{:T(128)} %get-tuple-element.97), kind=kOutput, calls=%fused_computation.3.clone.1 | convolution fusion | flops 19924279296 | bytes 60443136 | tf_op jit(solution)/shard_map/while/body/eval_jaxpr/td,vd->tv/dot_general | solution.py:17
  770.5 28.9 %multiply_reduce_fusion.2 = (f32[512]{0:T(512)S(1)}, f32[512,9496]{0,1:T(8,128)}) fusion(bf16[9496,2048]{1,0:T(8,128)(2,1)} %get-tuple-element.106, bf16[16,512,2048]{2,1,0:T(8,128)(2,1)} %get-tuple-element.105, s32[]{:T(128)} %get-tuple-element.97), kind=kOutput, calls=%fused_computation.3.clone.1 | convolution fusion | flops 19924279296 | bytes 60443136 | tf_op jit(solution)/shard_map/while/body/eval_jaxpr/td,vd->tv/dot_general | solution.py:17
  799.4 9.8 %exponential_reduce_fusion.2 = (f32[512]{0:T(512)S(1)}, f32[512]{0:T(512)S(1)}) fusion(f32[512,9496]{0,1:T(8,128)} %get-tuple-element.87, f32[512]{0:T(512)S(1)} %get-tuple-element.88, s32[512]{0:T(512)S(1)} %bitcast.47), kind=kLoop, calls=%fused_computation.2.clone.1 | loop fusion | flops 29170688 | bytes 19456000 | tf_op jit(solution)/shard_map/while/body/eval_jaxpr/reduce_sum | solution.py:19
  809.3 13.3 %all_to_all.5 = f32[16,3,512]{2,1,0:T(4,128)S(1)} all-to-all(f32[16,3,512]{2,1,0:T(4,128)S(1)} %get-tuple-element.29), channel_id=1, replica_groups=mesh['dp'=4,'tp'=16] {'tp'}, dimensions={0} | all-to-all | bytes 196608 | tf_op jit(solution)/shard_map/all_to_all | solution.py:40
  (47 shorter events, 46.2 us)
Async XLA Ops:
  7.2 181.9 %all-gather.5.cloned.1.call-start = ((), (), s32[]{:S(2)}) async-start(), calls=%async_computation.1 | async-start | bytes 35651584 | tf_op jit(solution)/shard_map/all_gather | solution.py:32
Sparse Core Ops, SparseCore 0:
  13.0 176.1 all-gather.4
where the time goes:
time: 832 us; the launch traced here: 830 us
  matrix products  462 us (56%)
  other arithmetic  164 us (20%)
  waiting for transfers between devices  153 us (18%)
  blocking collectives  36.2 us (4%)
  between operations  14.1 us (2%)
    dot_general x16, matrix products, shard_stats(): jnp.einsum('td,vd->tv', normed, table, preferred_element_type=jnp.float32)  462 us
    reduce_sum x16, other arithmetic, shard_stats(): exp_sum = jnp.sum(jnp.exp(logits - row_max[:, None]), axis=-1)  157 us
    all_gather x1, waiting for transfers between devices, local_part(): all_rows = lax.all_gather(normed, 'tp')  153 us
    all_gather x1, blocking collectives, local_part(): all_ids = lax.all_gather(target, 'tp') - shard_idx * shard_rows  22.9 us
  transfers between devices with their start and end apart: 1, of which 1 were waited for; matrix products, arithmetic and copies ran while one was open for 0% of the time, Pallas kernels for 0%

commit v1 on v0

v1 whole, which is shorter than its diff:
```python
import functools
import math

import jax
import jax.numpy as jnp
from jax import lax
from jax.experimental import pallas as pl
from jax.experimental.pallas import tpu as pltpu
from jax.sharding import PartitionSpec as P

NORM_EPS = 1e-5
OUT_SCALE = 0.5773502691896257
LOG2E = 1.0 / math.log(2.0)
LN2 = math.log(2.0)
PIECE = 72
CHUNK = 288
TRIP = 11 * CHUNK
COLS = 256
MESH = pl.DeviceIdType.MESH


def kernel(n_dev, hidden, gain, embed, target, log_prob, log_sum, blocks,
           tab, act, even, odd, tail, stats, ids, outbox, inbox, words,
           row_sem, save_sem, tab_sem, act_sem, recv_sem, ring_sem, pair_sem, word_out, word_in, box_out, box_in):
    rows, dim = embed.shape
    tok = hidden.shape[0]
    n_trip = pl.cdiv(rows, TRIP)
    pad = n_trip * TRIP - rows
    me = lax.axis_index("tp")
    chip, core = lax.div(me, 2), lax.rem(me, 2)
    n_chip = n_dev // 2
    way = 1 - 2 * core
    ahead = lax.rem(chip + way + n_chip, n_chip) * 2 + core
    pair = chip * 2 + 1 - core

    def owner(j):
        hop = lax.div(j + 2, 4)
        side = 1 - 2 * lax.rem(j, 2)
        at = lax.rem(chip - way * side * hop + n_chip, n_chip)
        late = lax.div(j + n_dev - 2, n_dev)
        return at * 2 + lax.rem(core + lax.div(j, 2) + lax.rem(j, 2) + late, 2)

    def send_block(src, slot, sem, dev):
        return pltpu.make_async_remote_copy(
            src_ref=src, dst_ref=blocks.at[slot], send_sem=sem, recv_sem=recv_sem.at[slot],
            device_id={"tp": dev}, device_id_type=MESH)

    def send_words(dev):
        return pltpu.make_async_remote_copy(
            src_ref=target, dst_ref=words.at[me], send_sem=word_out.at[dev], recv_sem=word_in.at[me],
            device_id={"tp": dev}, device_id_type=MESH)

    def recv_words(dev):
        return pltpu.make_async_remote_copy(
            src_ref=target, dst_ref=words.at[dev], send_sem=word_out.at[dev], recv_sem=word_in.at[dev],
            device_id={"tp": dev}, device_id_type=MESH)

    def send_stats(j, dev):
        return pltpu.make_async_remote_copy(
            src_ref=outbox.at[j], dst_ref=inbox.at[me], send_sem=box_out.at[j], recv_sem=box_in.at[me],
            device_id={"tp": dev}, device_id_type=MESH)

    def recv_stats(dev):
        return pltpu.make_async_remote_copy(
            src_ref=outbox.at[0], dst_ref=inbox.at[dev], send_sem=box_out.at[0], recv_sem=box_in.at[dev],
            device_id={"tp": dev}, device_id_type=MESH)

    def load_table(t, n):
        at = pl.ds(pl.multiple_of(t * TRIP, 8), n)
        return pltpu.make_async_copy(embed.at[at], tab.at[at], tab_sem.at[t])

    def load_act(j):
        return pltpu.make_async_copy(blocks.at[lax.rem(j, n_dev)], act.at[lax.rem(j, 2)], act_sem)

    def place(j):
        other = lax.div(lax.rem(j, n_dev) + n_dev - 1, n_dev)
        return other * lax.rem(j, 2) + 2 * (1 - other)

    def prepare(slot, dev):
        local = words[dev] - me * rows
        local = jnp.where((local >= 0) & (local < rows), local, -TRIP * n_trip)
        local = jnp.broadcast_to(local, (8, tok)) - lax.broadcasted_iota(jnp.int32, (8, tok), 0)
        ids[slot] = local.astype(jnp.float32)
        stats[slot, 0] = jnp.full((8, tok), -jnp.inf, jnp.float32)
        stats[slot, 1] = jnp.zeros((8, tok), jnp.float32)
        stats[slot, 2] = jnp.zeros((8, tok), jnp.float32)

    def finish(slot):
        part_max, part_sum, part_tgt = stats[slot, 0], stats[slot, 1], stats[slot, 2]
        top = jnp.max(part_max, axis=0, keepdims=True)
        total = jnp.sum(part_sum * jnp.exp2(part_max - top), axis=0, keepdims=True)
        tgt = jnp.sum(part_tgt, axis=0, keepdims=True)
        return top, total, tgt

    def fill(ref, at, values):
        for i, v in enumerate(values):
            ref[at, pl.ds(i, 1), :] = v

    def product(ref, at_zero, base, slot):
        at = pl.ds(pl.multiple_of(base, 16), CHUNK)
        ref[at_zero] = lax.dot_general(tab[at, :], act[slot], (((1,), (1,)), ((), ())),
                                       preferred_element_type=jnp.float32)

    def columns(slot):
        return [[stats[slot, i, :, c:c + COLS] for i in range(3)] for c in range(0, tok, COLS)]

    def keep(slot, vals):
        for q, val in enumerate(vals):
            for i in range(3):
                stats[slot, i, :, q * COLS:(q + 1) * COLS] = val[i]

    def epilogue(ref, at_zero, vals, slot, base, final):
        wait = 0.0
        for p in range(0, CHUNK, PIECE):
            for q, (top, total, tgt) in enumerate(vals):
                cols = slice(q * COLS, (q + 1) * COLS)
                word = (ids[slot, :, cols] - lax.convert_element_type(base, jnp.float32)) + wait
                scale = OUT_SCALE * LOG2E + wait
                raw = [ref[at_zero, i:i + 8, cols] for i in range(p, p + PIECE, 8)]
                log2 = [r * scale for r in raw]
                if final and p == CHUNK - PIECE:
                    for i in range(pad // 8):
                        log2[-1 - i] = jnp.where(base + (CHUNK - 8 * i) > rows, -jnp.inf, log2[-1 - i])
                new = jnp.maximum(top, functools.reduce(jnp.maximum, log2))
                terms = [jnp.exp2(v - new) for v in log2]
                total = total * jnp.exp2(top - new) + functools.reduce(jnp.add, terms)
                wait = total * 0.0
                for i, r in enumerate(raw):
                    tgt = jnp.where(word == float(p + 8 * i), r, tgt)
                vals[q] = [new, total, tgt]
        return vals

    def deliver(j):
        fill(outbox, j, finish(lax.rem(j, 2)))
        send_stats(j, owner(j)).start()

    barrier = pltpu.get_barrier_semaphore()
    for i in range(1, n_dev):
        pl.semaphore_signal(barrier, inc=1, device_id={"tp": lax.rem(me + i, n_dev)}, device_id_type=MESH)
    rows_in = pltpu.make_async_copy(hidden, act.at[0], row_sem)
    rows_in.start()
    for t in range(n_trip):
        load_table(t, min(TRIP, rows - t * TRIP)).start()
    words[me] = target[...]
    prepare(2, me)
    for i in range(3):
        stats[1, i] = jnp.zeros((8, tok), jnp.float32)
    ids[1] = jnp.zeros((8, tok), jnp.float32)
    rows_in.wait()

    def norm(i, _):
        at = pl.ds(pl.multiple_of(i * 16, 16), 16)
        x = act[0, at, :].astype(jnp.float32)
        mean_sq = jnp.mean(x * x, axis=-1, keepdims=True)
        act[0, at, :] = (x * lax.rsqrt(mean_sq + NORM_EPS) * gain[...]).astype(jnp.bfloat16)
        return 0

    lax.fori_loop(0, tok // 16, norm, 0, unroll=4)
    own_save = pltpu.make_async_copy(act.at[0], blocks.at[0], save_sem)
    own_pair = send_block(act.at[0], 1, pair_sem.at[0], pair)
    own_ring = send_block(act.at[0], 2, ring_sem.at[0], ahead)
    pl.semaphore_wait(barrier, n_dev - 1)
    own_pair.start()
    own_ring.start()
    own_save.start()
    for i in range(1, n_dev):
        send_words(lax.rem(me + i, n_dev)).start()
    tail[...] = jnp.zeros_like(tail)

    last = n_dev - 1
    n_step = n_dev * n_trip

    def fetch(k):
        send_block(blocks.at[0], k, pair_sem.at[0], pair).wait_recv()
        load_act(k).start()

    def step(g, _):
        h = g + lax.div(g + n_step - n_trip + 1, n_step)
        j, t = lax.div(h, n_trip), lax.rem(h, n_trip)
        slot, box = lax.rem(j, 2), place(j)

        for i in range(n_trip):
            @pl.when(g == (i if i < n_trip - 1 else 2 * n_trip - 2))
            def _(i=i):
                load_table(i, min(TRIP, rows - i * TRIP)).wait()

        get = lax.div(g, n_step)

        @pl.when((t == 0) & (j > 0))
        def _():
            load_act(j).wait()

            @pl.when(j < n_dev)
            def _():
                dev = owner(j)
                recv_words(dev).wait_recv()
                prepare(slot, dev)

        @pl.when(j == n_dev)
        def _():
            at = last % 2
            keep(at, epilogue(tail, get, columns(at), at, n_trip * TRIP - CHUNK, True))
            deliver(last)

        @pl.when(g == n_trip - 2)
        def _():
            fetch(1)
            send_block(blocks.at[1], 4, ring_sem.at[1], ahead).start()

        @pl.when(t == n_trip - 1)
        def _():
            @pl.when(j == 1)
            def _():
                own_pair.wait_send()
                own_ring.wait_send()
                own_save.wait()

            @pl.when(j > 1)
            def _():
                deliver(j - 1)

            @pl.when(j == last)
            def _():
                load_act(n_dev).start()

            @pl.when(j < last)
            def _():
                k = j + 1
                fetch(k)

                @pl.when(lax.rem(k, 2) == 0)
                def _():
                    send_block(blocks.at[k], k + 1, pair_sem.at[lax.div(k, 2)], pair).start()

                    @pl.when(k + 4 < n_dev)
                    def _():
                        send_block(blocks.at[k], k + 4, ring_sem.at[lax.div(k, 2) + 1], ahead).start()

        first = lax.div(n_trip - t, n_trip)
        after_own = lax.div(j + n_dev - 1, n_dev) - lax.div(j + n_dev - 2, n_dev)
        base = (t + lax.div(j, n_dev) * (n_trip - 1)) * TRIP
        before = first * (2 * after_own + (1 - after_own) * lax.rem(j + 1, 2)) + (1 - first) * box
        folded = first * (n_trip - after_own) * TRIP + (1 - first) * base - CHUNK
        put = lax.div(t, n_trip)
        product(even, put, base, slot)
        keep(before, epilogue(tail, get, columns(before), before, folded, True))
        vals = columns(box)
        refs = [even, odd] * (TRIP // CHUNK)
        refs[TRIP // CHUNK - 1] = tail
        for i in range(1, TRIP // CHUNK):
            product(refs[i], put, base + i * CHUNK, slot)
            vals = epilogue(refs[i - 1], get, vals, box, base + (i - 1) * CHUNK, False)
        keep(box, vals)
        return 0

    lax.fori_loop(0, n_step, step, 0)
    keep(2, epilogue(tail, 0, columns(2), 2, n_trip * TRIP - CHUNK, True))
    fill(inbox, me, finish(2))

    for i in range(1, n_dev):
        recv_stats(lax.rem(me + i, n_dev)).wait_recv()
    parts = [inbox[i] for i in range(n_dev)]
    top = functools.reduce(jnp.maximum, [p[0:1] for p in parts])
    total = functools.reduce(jnp.add, [p[1:2] * jnp.exp2(p[0:1] - top) for p in parts])
    tgt = functools.reduce(jnp.add, [p[2:3] for p in parts]) * OUT_SCALE
    norm_log = top * LN2 + jnp.log(total)
    log_sum[...] = norm_log
    log_prob[...] = tgt - norm_log
    for i in range(1, n_dev):
        send_words(lax.rem(me + i, n_dev)).wait_send()
        send_stats(i, pair).wait_send()
    for i in range(1, n_dev // 2):
        send_block(blocks.at[0], 0, pair_sem.at[i], pair).wait_send()
        if i < n_dev // 2 - 1:
            send_block(blocks.at[0], 0, ring_sem.at[i], ahead).wait_send()


def solution(mesh):
    n_dev = mesh.shape["tp"]
    row_spec = P(("dp", "tp"))

    def local_part(hidden, norm_scale, embed, target):
        tok, dim = hidden.shape
        rows = embed.shape[0]
        n_trip = pl.cdiv(rows, TRIP)
        dma = pltpu.SemaphoreType.DMA
        vmem = pl.BlockSpec(memory_space=pltpu.VMEM)
        anywhere = pl.BlockSpec(memory_space=pl.ANY)
        one = jax.ShapeDtypeStruct((1, tok), jnp.float32)
        log_prob, log_sum, _ = pl.pallas_call(
            functools.partial(kernel, n_dev),
            out_shape=(one, one, jax.ShapeDtypeStruct((n_dev, tok, dim), jnp.bfloat16)),
            in_specs=[anywhere, vmem, anywhere, vmem],
            out_specs=(vmem, vmem, anywhere),
            scratch_shapes=[
                pltpu.VMEM((n_trip * TRIP, dim), jnp.bfloat16),
                pltpu.VMEM((2, tok, dim), jnp.bfloat16),
                pltpu.VMEM((1, CHUNK, tok), jnp.float32),
                pltpu.VMEM((1, CHUNK, tok), jnp.float32),
                pltpu.VMEM((1, CHUNK, tok), jnp.float32),
                pltpu.VMEM((3, 3, 8, tok), jnp.float32),
                pltpu.VMEM((3, 8, tok), jnp.float32),
                pltpu.VMEM((n_dev, 8, tok), jnp.float32),
                pltpu.VMEM((n_dev, 8, tok), jnp.float32),
                pltpu.VMEM((n_dev, 1, tok), jnp.int32),
                dma, dma, dma((n_trip,)), dma, dma((n_dev,)), dma((n_dev // 2,)), dma((n_dev // 2,)),
                dma((n_dev,)), dma((n_dev,)), dma((n_dev,)), dma((n_dev,)),
            ],
            compiler_params=pltpu.CompilerParams(
                collective_id=0, has_side_effects=True, vmem_limit_bytes=60 * 1024 * 1024),
            name="head",
        )(hidden, norm_scale.reshape(1, dim), embed, target.reshape(1, tok))
        return log_prob.reshape(tok), log_sum.reshape(tok)

    return jax.shard_map(local_part, mesh=mesh,
                         in_specs=(P(("dp", "tp"), None), P(None), P("tp", None), row_spec),
                         out_specs=(row_spec, row_spec), check_vma=False)
```

time: 832 us -> 357 us (0.43)
  matrix products: 462 us -> 0 us
  Pallas kernels: 0 us -> 354 us
  other arithmetic: 164 us -> 0 us
  waiting for transfers between devices: 153 us -> 0 us
  blocking collectives: 36.2 us -> 0 us
  between operations: 14.1 us -> 0.64 us
    dot_general x16 -> x0, matrix products: 462 us -> none  [shard_stats(): jnp.einsum('td,vd->tv', normed, table, preferred_element_type=jnp.float32)]
    pallas_call x0 -> x1, Pallas kernels: none -> 354 us  [local_part(): pl.pallas_call(functools.partial(kernel, n_dev), out_shape=(one, one, jax...]
    reduce_sum x18 -> x0, other arithmetic: 159 us -> none  [the longest x16 157 us: shard_stats(): exp_sum = jnp.sum(jnp.exp(logits - row_max[:, None]), axis=-1)]
    all_gather x1 -> x0, waiting for transfers between devices: 153 us -> none  [local_part(): all_rows = lax.all_gather(normed, 'tp')]
    all_gather x1 -> x0, blocking collectives: 22.9 us -> none  [local_part(): all_ids = lax.all_gather(target, 'tp') - shard_idx * shard_rows]
    all_to_all x1 -> x0, blocking collectives: 13.3 us -> none  [local_part(): tok_stats = lax.all_to_all(tok_stats, 'tp', 0, 0, tiled=True)]
  transfers between devices with their start and end apart: 1 -> 0, of which waited for: 1 -> 0; matrix products, arithmetic and copies ran while one was open for 0% -> 0% of each run, Pallas kernels for 0% -> 0%
where the time goes in v1:
time: 357 us
  Pallas kernels  354 us (99%)
    pallas_call x1, Pallas kernels, local_part(): pl.pallas_call(functools.partial(kernel, n_dev), out_shape=(one, one, jax...  354 us

profile of v1, /device:TPU:21, one launch (start us, length us, event | category | flops | bytes accessed | tf_op | source)
XLA Modules:
  0.0 356.9 jit_solution(10681287100459216289)
XLA Ops:
  0.6 353.7 %head.1 = (f32[1,512]{1,0:T(1,128)}, f32[1,512]{1,0:T(1,128)}, bf16[16,512,2048]{2,1,0:T(8,128)(2,1)}) custom-call(bf16[512,2048]{1,0:T(8,128)(2,1)} %hidden.1, f32[1,2048]{1,0:T(1,128)} %bitcast.4, bf16[9496,2048]{1,0:T(8,128)(2,1)} %embed.1, s32[1,512]{1,0:T(1,128)} %bitcast.5), custom_call_target="tpu_custom_call" | custom-call | tf_op jit(solution)/shard_map/head/pallas_call | solution.py:290
  354.3 1.3 copy.8
  355.6 1.3 copy.9
